TPU v7x, 32 devices: a whole 2x2x4 slice. The times are simulated.
32 devices in a mesh: scen: 16 (over z, y, x), fac: 2 (over core).
Axes of the slice: x: 2, y: 2, z: 4, core: 2. Of those that a mesh axis runs over, the one named last changes fastest.
Arguments:
- scenario_pnl: float32 [16384, 2048], P('scen', 'fac'), may hold values from -300 to 300
Outputs:
- covariance: float32 [2048, 2048], P('scen', 'fac')
- factor_means: float32 [2048], P('fac')
All inputs are finite; a program needn't handle non-finite values.
Results may differ from a plain program's by a relative error of at most 0.0003.
Values sent between devices are 32-bit elements; how exact they have to be, the bound alone decides.
A program may use at most 64 MiB of HBM per device.

v0:
```python
import functools

import jax
import jax.numpy as jnp
from jax import lax
from jax.experimental import pallas as pl
from jax.experimental.pallas import tpu as pltpu
from jax.sharding import PartitionSpec as P

MESH = pl.DeviceIdType.MESH
LOADS = 4
TILE = 64


def block_gram(left, right):
    return lax.dot_general(
        left,
        right,
        (((0,), (0,)), ((), ())),
        precision=lax.Precision.HIGHEST,
        preferred_element_type=jnp.float32,
    )


def on_device(scenario_pnl):
    rows_here = scenario_pnl.shape[0]
    total_rows = rows_here * lax.axis_size("scen")
    local_sums = jnp.sum(scenario_pnl, axis=0)
    total_sums = lax.psum(local_sums, "scen")
    factor_means = total_sums / total_rows
    local_means = local_sums / rows_here
    data = scenario_pnl - local_means[None, :]
    partial_value = block_gram(lax.all_gather(data, "fac", axis=1, tiled=True), data)
    owned = lax.psum_scatter(partial_value, "scen", scatter_dimension=0, tiled=True)
    gathered = lax.all_gather(local_means, ("scen", "fac"), axis=0, tiled=True)
    spread_rows = gathered.reshape(lax.axis_size("scen"), -1)
    deviations = spread_rows - jnp.mean(spread_rows, axis=0, keepdims=True)
    owned_rows = owned.shape[0]
    column_width = owned.shape[1]
    row_part = lax.dynamic_slice_in_dim(
        deviations, lax.axis_index("scen") * owned_rows, owned_rows, 1
    )
    column_part = lax.dynamic_slice_in_dim(
        deviations, lax.axis_index("fac") * column_width, column_width, 1
    )
    owned = owned + rows_here * block_gram(row_part, column_part)
    covariance = owned / (total_rows - 1)
    return (covariance, factor_means)


def kernel(
    n, x_hbm, cov_ref, mean_ref,
    x_vm, other, hi_w, lo_w, hi_o, lo_o,
    send1, keep1, recv1, send2, recv2, zsend, zrecv,
    turned, landed, sums_own, sums_oth, dev_w, dev_o,
    load_sem, pair_s, pair_r, s1_s, s1_r, s2_s, s2_r, z_s, z_r, t_s, t_r,
    m_s, m_r, mo_s, mo_r,
):
    rows, width = x_hbm.shape
    half = n // 2
    block = width // half
    near, far = half // 2 + 1, half // 2
    depth = n // 4
    zh = depth // 2
    total_rows = rows * n

    s = lax.axis_index("scen")
    c = lax.axis_index("fac")
    z, y, x = s // 4, (s // 2) % 2, s % 2
    first = x * (1 - c) + y * c
    second = y * (1 - c) + x * c
    peer1 = s + (1 - 2 * x) * (1 - c) + (2 - 4 * y) * c
    peer2 = s + (2 - 4 * y) * (1 - c) + (1 - 2 * x) * c

    barrier = pltpu.get_barrier_semaphore()
    me = s * 2 + c

    part = rows // LOADS
    loads = []
    for i in range(LOADS):
        at = pl.ds(i * part, part)
        load = pltpu.make_async_copy(x_hbm.at[at], x_vm.at[at], load_sem.at[i])
        load.start()
        loads.append(load)

    def greet(d, carry):
        p = (me + d) % (2 * n)
        pl.semaphore_signal(barrier, inc=1, device_id=(p // 2, p % 2), device_id_type=MESH)
        return carry

    lax.fori_loop(1, 2 * n, greet, 0)

    def sums_of(ref, start, count, acc):
        def add(i, acc):
            at = pl.multiple_of(start + i * TILE, TILE)
            return acc + jnp.sum(ref[pl.ds(at, TILE), :].reshape(TILE // 8, 8, width), axis=0)

        return lax.fori_loop(0, count // TILE, add, acc)

    acc = jnp.zeros((8, width), jnp.float32)
    for i in range(LOADS):
        loads[i].wait()
        acc = sums_of(x_vm, i * part, part, acc)
    local_sum = jnp.sum(acc, axis=0, keepdims=True)
    sums_own[s] = local_sum
    local_mean = local_sum / rows
    mid = width // 2

    def split_own(i, carry):
        at = pl.ds(pl.multiple_of(i * TILE, TILE), TILE)
        data = x_vm[at, :] - local_mean
        hi = data.astype(jnp.bfloat16)
        lo = (data - hi.astype(jnp.float32)).astype(jnp.bfloat16)
        hi_w[at, :width] = hi
        lo_w[at, :width] = lo
        hi_w[at, width:] = hi[:, :mid]
        lo_w[at, width:] = lo[:, :mid]
        return carry

    lax.fori_loop(0, rows // TILE, split_own, 0)

    def split_other():
        acc = sums_of(other, 0, rows, jnp.zeros((8, width), jnp.float32))
        mean = jnp.sum(acc, axis=0, keepdims=True) / rows

        def body(i, carry):
            at = pl.ds(pl.multiple_of(i * TILE, TILE), TILE)
            data = other[at, :] - mean
            hi = data.astype(jnp.bfloat16)
            hi_o[at, :] = hi
            lo_o[at, :] = (data - hi.astype(jnp.float32)).astype(jnp.bfloat16)
            return carry

        lax.fori_loop(0, rows // TILE, body, 0)

    def gram(left, right):
        return lax.dot_general(
            left, right, (((0,), (0,)), ((), ())), preferred_element_type=jnp.float32
        )

    def slot_of(k):
        turn = (k + z) % zh
        return c * zh + turn if k < zh else (1 - c) * zh + turn

    def width_of(k):
        return (near if k < zh else far) * block

    def compute(k, side, dst, send=False):
        own = k < zh
        wide = width_of(k)
        hi_l, lo_l = (hi_w, lo_w) if own else (hi_o, lo_o)

        def body(j, carry):
            b = (1 - second) + j * (2 * second - 1)
            px = side * (1 - c) + b * c
            py = b * (1 - c) + side * c
            r = (slot_of(k) * 4 + py * 2 + px) % half
            rows_at = pl.ds(pl.multiple_of(r * block, block), block)
            start = r if own else r + c
            cols_at = pl.ds(pl.multiple_of(start * block, block), wide)
            lh, ll = hi_l[:, rows_at], lo_l[:, rows_at]
            rh, rl = hi_w[:, cols_at], lo_w[:, cols_at]
            dst[k, j, :, :wide] = gram(lh, rh) + (gram(lh, rl) + gram(ll, rh))
            if send:
                stage1(k, j).start()
            return carry

        lax.fori_loop(0, 2, body, 0)

    def remote(src, dst, send, recv, scen, fac):
        return pltpu.make_async_remote_copy(
            src_ref=src, dst_ref=dst, send_sem=send, recv_sem=recv,
            device_id=(scen, fac), device_id_type=MESH,
        )

    def stage1(k, j):
        w = width_of(k)
        return remote(
            send1.at[k, j, :, :w], recv1.at[k, j, :, :w], s1_s.at[k, j], s1_r.at[k, j], peer1, c
        )

    def stage2(k):
        w = width_of(k)
        return remote(send2.at[k, :, :w], recv2.at[k, :, :w], s2_s.at[k], s2_r.at[k], peer2, c)

    def stage3(k):
        w = width_of(k)
        t = slot_of(k)
        place = (z - t + depth - 1) % depth
        return remote(
            zsend.at[k, :, :w], zrecv.at[place, :, :w], z_s.at[k], z_r.at[place],
            t * 4 + y * 2 + x, c,
        )

    def relay1(k):
        w = width_of(k)
        stage1(k, 0).wait_recv()
        send2[k, :, :w] = keep1[k, 0, :, :w] + recv1[k, 0, :, :w]
        stage2(k).start()

    def relay2(k):
        w = width_of(k)
        stage1(k, 1).wait_recv()
        stage2(k).wait_recv()
        zsend[k, :, :w] = keep1[k, 1, :, :w] + recv1[k, 1, :, :w] + recv2[k, :, :w]

        @pl.when(slot_of(k) != z)
        def _():
            stage3(k).start()

    pl.semaphore_wait(barrier, 2 * n - 1)
    compute(0, 1 - first, send1, True)
    pair = remote(x_vm, other, pair_s, pair_r, s, 1 - c)
    pair.start()

    def mean_copy(d):
        p = (s + d) % n
        return remote(sums_own.at[s], sums_own.at[s], m_s.at[d], m_r.at[d], p, c)

    for d in range(1, n):
        mean_copy(d).start()

    compute(0, first, keep1)
    compute(1, 1 - first, send1, True)
    compute(1, first, keep1)

    for d in range(1, n):
        q = (s - d + n) % n
        remote(sums_own.at[q], sums_own.at[q], m_s.at[d], m_r.at[d], q, c).wait_recv()
    swap = remote(sums_own, sums_oth, mo_s, mo_r, s, 1 - c)
    swap.start()

    relay1(0)
    pair.wait_recv()
    split_other()
    compute(2, 1 - first, send1, True)
    relay1(1)
    compute(2, first, keep1)
    compute(3, 1 - first, send1, True)
    relay2(0)
    compute(3, first, keep1)

    def deviations(ref):
        sums = ref[...].reshape(n, width)
        total = jnp.sum(sums, axis=0, keepdims=True)
        return sums / rows - total / total_rows, total / total_rows

    dev, means = deviations(sums_own)
    mean_ref[...] = means
    dev_w[:, :width] = dev
    dev_w[:, width:] = dev[:, :mid]
    swap.wait_recv()
    dev_o[...] = deviations(sums_oth)[0]

    relay1(2)
    relay2(1)
    relay1(3)
    relay2(2)
    relay2(3)

    r = s % half

    def turn_copy(own, d):
        if own:
            return remote(
                turned.at[d], landed.at[d], t_s.at[d], t_r.at[d], c * half + (r + d) % half, c
            )
        return remote(
            turned.at[d], landed.at[d], t_s.at[d], t_r.at[d],
            c * half + (r + c + d) % half, 1 - c,
        )

    def finish(own):
        count = near if own else far
        w = count * block
        for k in (range(zh) if own else range(zh, 2 * zh)):
            @pl.when(slot_of(k) == z)
            def _():
                for place in range(depth - 1):
                    remote(
                        zsend.at[k, :, :w], zrecv.at[place, :, :w], z_s.at[k], z_r.at[place],
                        s, 1 - c,
                    ).wait_recv()
                left = (dev_w if own else dev_o)[:, pl.ds(pl.multiple_of(r * block, block), block)]
                start = r if own else r + c
                shift = block_gram(
                    left, dev_w[:, pl.ds(pl.multiple_of(start * block, block), w)]
                )
                value = zsend[k, :, :w]
                for place in range(depth - 1):
                    value = value + zrecv[place, :, :w]
                value = (value + rows * shift) / (total_rows - 1)
                turns = range(1, near - 1) if own else range(far)
                for d in turns:
                    turned[d] = value[:, d * block:(d + 1) * block].T
                    turn_copy(own, d).start()
                for d in range(count):
                    q = (start + d) % half
                    cov_ref[:, pl.ds(pl.multiple_of(q * block, block), block)] = value[
                        :, d * block:(d + 1) * block
                    ]
                for d in turns:
                    turn_copy(own, d).wait_recv()
                    q = (r - d + half) % half if own else (r - (1 - c) - d + 2 * half) % half
                    cov_ref[:, pl.ds(pl.multiple_of(q * block, block), block)] = landed[d]
                for d in turns:
                    turn_copy(own, d).wait_send()

    finish(True)
    finish(False)

    pair.wait_send()
    swap.wait_send()
    for d in range(1, n):
        mean_copy(d).wait_send()
    for k in range(2 * zh):
        stage1(k, 0).wait_send()
        stage1(k, 1).wait_send()
        stage2(k).wait_send()

        @pl.when(slot_of(k) != z)
        def _():
            stage3(k).wait_send()


def by_kernel(n, scenario_pnl):
    rows, width = scenario_pnl.shape
    half = n // 2
    block = width // half
    near = half // 2 + 1
    depth = n // 4
    f32, bf16 = jnp.float32, jnp.bfloat16
    dma = pltpu.SemaphoreType.DMA
    covariance, factor_means = pl.pallas_call(
        functools.partial(kernel, n),
        out_shape=(
            jax.ShapeDtypeStruct((block, width), f32),
            jax.ShapeDtypeStruct((1, width), f32),
        ),
        in_specs=[pl.BlockSpec(memory_space=pl.ANY)],
        out_specs=[pl.BlockSpec(memory_space=pltpu.VMEM)] * 2,
        scratch_shapes=[
            pltpu.VMEM((rows, width), f32),
            pltpu.VMEM((rows, width), f32),
            pltpu.VMEM((rows, width + width // 2), bf16),
            pltpu.VMEM((rows, width + width // 2), bf16),
            pltpu.VMEM((rows, width), bf16),
            pltpu.VMEM((rows, width), bf16),
            pltpu.VMEM((depth, 2, block, near * block), f32),
            pltpu.VMEM((depth, 2, block, near * block), f32),
            pltpu.VMEM((depth, 2, block, near * block), f32),
            pltpu.VMEM((depth, block, near * block), f32),
            pltpu.VMEM((depth, block, near * block), f32),
            pltpu.VMEM((depth, block, near * block), f32),
            pltpu.VMEM((depth - 1, block, near * block), f32),
            pltpu.VMEM((near - 1, block, block), f32),
            pltpu.VMEM((near - 1, block, block), f32),
            pltpu.VMEM((n, 1, width), f32),
            pltpu.VMEM((n, 1, width), f32),
            pltpu.VMEM((n, width + width // 2), f32),
            pltpu.VMEM((n, width), f32),
            dma((LOADS,)),
            dma, dma,
            dma((depth, 2)), dma((depth, 2)),
            dma((depth,)), dma((depth,)),
            dma((depth,)), dma((depth - 1,)),
            dma((near - 1,)), dma((near - 1,)),
            dma((n,)), dma((n,)),
            dma, dma,
        ],
        compiler_params=pltpu.CompilerParams(
            collective_id=0, has_side_effects=True, vmem_limit_bytes=60 * 1024 * 1024
        ),
    )(scenario_pnl)
    return covariance, factor_means.reshape(width)


def solution(mesh):
    n, cores = mesh.shape["scen"], mesh.shape["fac"]

    def body(scenario_pnl):
        rows, width = scenario_pnl.shape
        fits = cores == 2 and n % 16 == 0 and n // 4 == 4 and width % (n * 64) == 0
        if fits and rows % (LOADS * TILE) == 0:
            return by_kernel(n, scenario_pnl)
        return on_device(scenario_pnl)

    return jax.shard_map(
        body,
        mesh=mesh,
        in_specs=(P("scen", "fac"),),
        out_specs=(P("scen", "fac"), P("fac")),
        check_vma=False,
    )
```

profile of v0, /device:TPU:1, one launch (start us, length us, event | category | flops | bytes accessed | tf_op | source)
XLA Modules:
  0.0 70.9 jit_solution(17153724880274529427)
XLA Ops:
  0.6 67.1 %shard_map.30 = (f32[128,1024]{1,0:T(8,128)}, f32[1,1024]{1,0:T(1,128)}) custom-call(f32[1024,1024]{1,0:T(8,128)} %x_hbm.1), custom_call_target="tpu_custom_call" | custom-call | tf_op jit(solution)/shard_map/pallas_call | solution.py:334
  67.7 1.9 %copy.5 = f32[128,1024]{1,0:T(8,128)} copy(f32[128,1024]{1,0:T(8,128)} %get-tuple-element.8) | data formatting | bytes 1048576
  69.6 1.3 %copy.6 = f32[1024]{0:T(1024)} copy(f32[1024]{0:T(1024)} %bitcast.1) | data formatting | bytes 8192
where the time goes:
time: 71.1 us; the launch traced here: 70.9 us
  Pallas kernels  67.1 us (94%)
  local copies, waits for them, and re-layouts  3.15 us (4%)
    pallas_call x1, Pallas kernels, by_kernel(): pl.pallas_call(functools.partial(kernel, n), out_shape=(jax.ShapeDtypeStr...  67.1 us
    unnamed x2, local copies, waits for them, and re-layouts  3.15 us

commit v1 on v0

--- a/solution.py
+++ b/solution.py
@@ -333,10 +333,7 @@
     dma = pltpu.SemaphoreType.DMA
     covariance, factor_means = pl.pallas_call(
         functools.partial(kernel, n),
-        out_shape=(
-            jax.ShapeDtypeStruct((block, width), f32),
-            jax.ShapeDtypeStruct((1, width), f32),
-        ),
+        out_shape=(pltpu.VMEM((block, width), f32), pltpu.VMEM((1, width), f32)),
         in_specs=[pl.BlockSpec(memory_space=pl.ANY)],
         out_specs=[pl.BlockSpec(memory_space=pltpu.VMEM)] * 2,
         scratch_shapes=[

time: 71.1 us -> 68.5 us (0.963)
  local copies, waits for them, and re-layouts: 3.15 us -> 1.39 us
  Pallas kernels: 67.1 us -> 66.3 us
    unnamed x2, local copies, waits for them, and re-layouts: 3.15 us -> 1.39 us
    pallas_call x1, Pallas kernels: 67.1 us -> 66.3 us  [by_kernel(): pl.pallas_call(functools.partial(kernel, n), out_shape=(pltpu.VMEM((block...]
where the time goes in v1:
time: 68.5 us; the launch traced here: 68.3 us
  Pallas kernels  66.3 us (97%)
  local copies, waits for them, and re-layouts  1.39 us (2%)
    pallas_call x1, Pallas kernels, by_kernel(): pl.pallas_call(functools.partial(kernel, n), out_shape=(pltpu.VMEM((block...  66.3 us
    unnamed x2, local copies, waits for them, and re-layouts  1.39 us

profile of v1, /device:TPU:1, one launch (start us, length us, event | category | flops | bytes accessed | tf_op | source)
XLA Modules:
  0.0 68.3 jit_solution(14322924624130748248)
XLA Ops:
  0.6 66.3 %shard_map.30 = (f32[128,1024]{1,0:T(8,128)S(1)}, f32[1,1024]{1,0:T(1,128)S(1)}) custom-call(f32[1024,1024]{1,0:T(8,128)} %x_hbm.1), custom_call_target="tpu_custom_call" | custom-call | tf_op jit(solution)/shard_map/pallas_call | solution.py:334
  66.9 0.8 %copy.5 = f32[128,1024]{1,0:T(8,128)} copy(f32[128,1024]{1,0:T(8,128)S(1)} %get-tuple-element.6) | data formatting | bytes 1048576
  67.7 0.6 copy.6

commit v2 on v1

v2 whole, which is shorter than its diff:
```python
import functools

import jax
import jax.numpy as jnp
from jax import lax
from jax.experimental import pallas as pl
from jax.experimental.pallas import tpu as pltpu
from jax.sharding import PartitionSpec as P

MESH = pl.DeviceIdType.MESH
LOADS = 4
TILE = 64


def block_gram(left, right):
    return lax.dot_general(
        left,
        right,
        (((0,), (0,)), ((), ())),
        precision=lax.Precision.HIGHEST,
        preferred_element_type=jnp.float32,
    )


def on_device(scenario_pnl):
    rows_here = scenario_pnl.shape[0]
    total_rows = rows_here * lax.axis_size("scen")
    local_sums = jnp.sum(scenario_pnl, axis=0)
    total_sums = lax.psum(local_sums, "scen")
    factor_means = total_sums / total_rows
    local_means = local_sums / rows_here
    data = scenario_pnl - local_means[None, :]
    partial_value = block_gram(lax.all_gather(data, "fac", axis=1, tiled=True), data)
    owned = lax.psum_scatter(partial_value, "scen", scatter_dimension=0, tiled=True)
    gathered = lax.all_gather(local_means, ("scen", "fac"), axis=0, tiled=True)
    spread_rows = gathered.reshape(lax.axis_size("scen"), -1)
    deviations = spread_rows - jnp.mean(spread_rows, axis=0, keepdims=True)
    owned_rows = owned.shape[0]
    column_width = owned.shape[1]
    row_part = lax.dynamic_slice_in_dim(
        deviations, lax.axis_index("scen") * owned_rows, owned_rows, 1
    )
    column_part = lax.dynamic_slice_in_dim(
        deviations, lax.axis_index("fac") * column_width, column_width, 1
    )
    owned = owned + rows_here * block_gram(row_part, column_part)
    covariance = owned / (total_rows - 1)
    return (covariance, factor_means)


def kernel(
    n, x_hbm, cov_ref, mean_ref,
    x_vm, other, hi, lo,
    send1, keep1, recv1, send2, recv2, zsend, zrecv, xrecv,
    turned, landed, sums_own, sums_oth, pair_sum, dev_a,
    load_sem, pair_s, pair_r, ps_s, ps_r, s1_s, s1_r, s2_s, s2_r, z_s, z_r, x_s, x_r,
    t_s, t_r, m_s, m_r, mo_s, mo_r,
):
    rows, width = x_hbm.shape
    half = n // 2
    block = width // half
    quads, parts = n // 4, 2
    wide = half // 4 * block
    extra = parts * quads
    wrapped = width + width // 2
    total_rows = rows * n

    s = lax.axis_index("scen")
    c = lax.axis_index("fac")
    z, y, x = s // 4, (s // 2) % 2, s % 2
    first = x * (1 - c) + y * c
    second = y * (1 - c) + x * c
    peer1 = s + (1 - 2 * x) * (1 - c) + (2 - 4 * y) * c
    peer2 = s + (2 - 4 * y) * (1 - c) + (1 - 2 * x) * c
    odd, own_z = z % 2, 1 - (z // 2 - c) * (z // 2 - c)

    barrier = pltpu.get_barrier_semaphore()
    me = s * 2 + c

    part = rows // LOADS
    loads = []
    for i in range(LOADS):
        at = pl.ds(i * part, part)
        load = pltpu.make_async_copy(x_hbm.at[at], x_vm.at[at], load_sem.at[i])
        load.start()
        loads.append(load)

    for d in range(1, 2 * n):
        p = (me + d) % (2 * n)
        pl.semaphore_signal(barrier, inc=1, device_id=(p // 2, p % 2), device_id_type=MESH)

    def sums_of(ref, start, count, acc):
        def add(i, acc):
            at = pl.multiple_of(start + i * TILE, TILE)
            return acc + jnp.sum(ref[pl.ds(at, TILE), :].reshape(TILE // 8, 8, width), axis=0)

        return lax.fori_loop(0, count // TILE, add, acc)

    acc = jnp.zeros((8, width), jnp.float32)
    for i in range(LOADS):
        loads[i].wait()
        acc = sums_of(x_vm, i * part, part, acc)
    local_sum = jnp.sum(acc, axis=0, keepdims=True)
    sums_own[s] = local_sum
    mid = width // 2

    def split(ref, mean, base, start, count, wrap):
        def body(i, carry):
            at = pl.ds(pl.multiple_of(start + i * TILE, TILE), TILE)
            data = ref[at, :] - mean
            high = data.astype(jnp.bfloat16)
            low = (data - high.astype(jnp.float32)).astype(jnp.bfloat16)
            hi[at, base:base + width] = high
            lo[at, base:base + width] = low
            if wrap:
                hi[at, width:wrapped] = high[:, :mid]
                lo[at, width:wrapped] = low[:, :mid]
            return carry

        lax.fori_loop(0, count // TILE, body, 0)

    split(x_vm, local_sum / rows, 0, 0, rows, True)

    def gram(left, right):
        return lax.dot_general(
            left, right, (((0,), (0,)), ((), ())), preferred_element_type=jnp.float32
        )

    def slot_of(k):
        near = (z + 1 - 2 * odd, 2 * (1 - c) + odd, 3 - 2 * c - odd, z)[k]
        far = (2 * c + odd, 2 * c + 1 - odd, z + 1 - 2 * odd, z)[k]
        return own_z * near + (1 - own_z) * far

    def width_of(t):
        return block if t == extra else wide

    def strip(t, px, py):
        if t == extra:
            r = py * 2 + px
            return r, r + half // 2
        to = slot_of(t % quads)
        r = (to * 4 + py * 2 + px) % half
        own = 1 - (to // 2 - c) * (to // 2 - c)
        return r + (1 - own) * (wrapped // block), r + (1 - own) * c + t // quads * (wide // block)

    def lanes(start, count):
        return pl.ds(pl.multiple_of(start * block, block), count)

    def compute(k, side, dst, send=False):
        pieces = (extra,) if k == quads else (k, quads + k)
        count = sum(width_of(t) for t in pieces)

        def body(j, carry):
            b = (1 - second) + j * (2 * second - 1)
            px, py = side * (1 - c) + b * c, b * (1 - c) + side * c
            left, right = strip(pieces[0], px, py)
            rows_at, cols_at = lanes(left, block), lanes(right, count)
            lh, ll = hi[:, rows_at], lo[:, rows_at]
            rh, rl = hi[:, cols_at], lo[:, cols_at]
            value = gram(lh, rh) + (gram(lh, rl) + gram(ll, rh))
            for t in pieces:
                w = width_of(t)
                at = (t // quads) * wide % count
                dst[t, j, :, :w] = value[:, at:at + w]
            if send:
                stage1(pieces[0], j).start()
            return carry

        lax.fori_loop(0, 2, body, 0)

    def remote(src, dst, send, recv, scen, fac):
        return pltpu.make_async_remote_copy(
            src_ref=src, dst_ref=dst, send_sem=send, recv_sem=recv,
            device_id=(scen, fac), device_id_type=MESH,
        )

    def stage1(t, j):
        w = width_of(t)
        return remote(
            send1.at[t, j, :, :w], recv1.at[t, j, :, :w], s1_s.at[t, j], s1_r.at[t, j], peer1, c
        )

    def stage2(t):
        w = width_of(t)
        return remote(send2.at[t, :, :w], recv2.at[t, :, :w], s2_s.at[t], s2_r.at[t], peer2, c)

    def stage3(t):
        to = slot_of(t % quads)
        place = (z - to + quads - 1) % quads
        return remote(
            zsend.at[t], zrecv.at[t // quads, place], z_s.at[t], z_r.at[t // quads, place],
            to * 4 + y * 2 + x, c,
        )

    def stage3_extra(e):
        to = 2 * c + e
        place = (z - to + quads - 1) % quads
        return remote(
            zsend.at[extra, :, :block], xrecv.at[place], x_s.at[e], x_r.at[place],
            to * 4 + y * 2 + x, c,
        )

    def relay1(t):
        w = width_of(t)
        stage1(t, 0).wait_recv()
        send2[t, :, :w] = keep1[t, 0, :, :w] + recv1[t, 0, :, :w]
        stage2(t).start()

    def relay2(t):
        w = width_of(t)
        stage1(t, 1).wait_recv()
        stage2(t).wait_recv()
        zsend[t, :, :w] = keep1[t, 1, :, :w] + recv1[t, 1, :, :w] + recv2[t, :, :w]
        if t == extra:
            for e in range(2):
                @pl.when(2 * c + e != z)
                def _():
                    stage3_extra(e).start()
        elif t % quads < quads - 1:
            stage3(t).start()

    def send_stage(t):
        for j in range(2):
            stage1(t, j).start()

    def pair_copy(i):
        at = pl.ds(i * part, part)
        return remote(x_vm.at[at], other.at[at], pair_s.at[i], pair_r.at[i], s, 1 - c)

    def mean_copy(d):
        p = (s + d) % n
        return remote(sums_own.at[s], sums_own.at[s], m_s.at[d], m_r.at[d], p, c)

    pl.semaphore_wait(barrier, 2 * n - 1)
    pair_mean = remote(sums_own.at[s], pair_sum, ps_s, ps_r, s, 1 - c)
    pair_mean.start()
    for i in range(LOADS):
        pair_copy(i).start()
    compute(quads, 1 - first, send1, True)
    compute(0, 1 - first, send1, True)
    for d in range(1, n):
        mean_copy(d).start()
    send_stage(quads)
    compute(quads, first, keep1)
    compute(0, first, keep1)
    relay1(extra)

    pair_mean.wait_recv()
    pair_mean_value = pair_sum[...] / rows
    for i in range(LOADS):
        pair_copy(i).wait_recv()
        split(other, pair_mean_value, wrapped, i * part, part, False)

    compute(1, 1 - first, send1, True)
    relay1(0)
    compute(1, first, keep1)
    compute(2, 1 - first, send1, True)
    relay2(extra)
    compute(2, first, keep1)
    relay1(quads)
    compute(3, 1 - first, send1, True)
    for t in range(quads + 1, 2 * quads):
        send_stage(t)
    compute(3, first, keep1)
    relay2(0)
    relay1(1)
    for d in range(1, n):
        q = (s - d + n) % n
        remote(sums_own.at[q], sums_own.at[q], m_s.at[d], m_r.at[d], q, c).wait_recv()
    swap = remote(sums_own, sums_oth, mo_s, mo_r, s, 1 - c)
    swap.start()
    relay2(quads)
    relay1(2)
    relay2(1)
    relay1(3)
    relay2(2)

    def deviations(ref):
        sums = ref[...].reshape(n, width)
        total = jnp.sum(sums, axis=0, keepdims=True)
        return sums / rows - total / total_rows, total / total_rows

    dev, means = deviations(sums_own)
    mean_ref[...] = means
    dev_a[:, :width] = dev
    dev_a[:, width:wrapped] = dev[:, :mid]
    swap.wait_recv()
    dev_a[:, wrapped:] = deviations(sums_oth)[0]

    relay1(quads + 1)
    relay2(3)

    r = s % half
    start = r + (1 - own_z) * c

    def put(q, value):
        cov_ref[:, lanes(q % half, block)] = value

    def turn_copy(d):
        return remote(
            turned.at[d], landed.at[d], t_s.at[d], t_r.at[d],
            c * half + (start + d) % half, own_z * c + (1 - own_z) * (1 - c),
        )

    def mirrored(d, act):
        if d:
            act()
        else:
            pl.when(own_z == 0)(act)

    def finish(p):
        t = p * quads + quads - 1
        for place in range(quads - 1):
            remote(
                zsend.at[t], zrecv.at[p, place], z_s.at[t], z_r.at[p, place], s, 1 - c
            ).wait_recv()
        left, right = strip(t, x, y)
        shift = block_gram(dev_a[:, lanes(left, block)], dev_a[:, lanes(right, wide)])
        value = zsend[t]
        for place in range(quads - 1):
            value = value + zrecv[p, place]
        value = (value + rows * shift) / (total_rows - 1)
        each = wide // block
        for i in range(each):
            d = p * each + i
            turned[d] = value[:, i * block:(i + 1) * block].T
            mirrored(d, turn_copy(d).start)
        for i in range(each):
            put(start + p * each + i, value[:, i * block:(i + 1) * block])

    def land(p):
        for d in range(p * (wide // block), (p + 1) * (wide // block)):
            def arrive():
                turn_copy(d).wait_recv()
                put(r - (1 - own_z) * (1 - c) - d + 2 * half, landed[d])

            mirrored(d, arrive)

    def finish_extra():
        @pl.when(own_z == 1)
        def _():
            for place in range(quads - 1):
                remote(
                    zsend.at[extra, :, :block], xrecv.at[place], x_s.at[0], x_r.at[place], s, 1 - c
                ).wait_recv()
            left, right = strip(extra, x, y)
            shift = block_gram(dev_a[:, lanes(left, block)], dev_a[:, lanes(right, block)])
            value = zsend[extra, :, :block]
            for place in range(quads - 1):
                value = value + xrecv[place]
            value = (value + rows * shift) / (total_rows - 1)

            @pl.when(odd == 0)
            def _():
                put(r + half // 2, value)

            @pl.when(odd == 1)
            def _():
                put(r + half // 2, value.T)

    relay1(quads + 2)
    relay2(quads + 1)
    relay1(quads + 3)
    relay2(quads + 2)
    finish(0)
    finish_extra()
    relay2(quads + 3)
    finish(1)
    land(0)
    land(1)

    pair_mean.wait_send()
    for i in range(LOADS):
        pair_copy(i).wait_send()
    swap.wait_send()
    for d in range(1, n):
        mean_copy(d).wait_send()
    for d in range(half // 2):
        mirrored(d, turn_copy(d).wait_send)
    for t in range(extra + 1):
        stage1(t, 0).wait_send()
        stage1(t, 1).wait_send()
        stage2(t).wait_send()
        if t == extra:
            for e in range(2):
                @pl.when(2 * c + e != z)
                def _():
                    stage3_extra(e).wait_send()
        elif t % quads < quads - 1:
            stage3(t).wait_send()


def by_kernel(n, scenario_pnl):
    rows, width = scenario_pnl.shape
    half = n // 2
    block = width // half
    wide = half // 4 * block
    tasks = 2 * (n // 4) + 1
    f32, bf16 = jnp.float32, jnp.bfloat16
    dma = pltpu.SemaphoreType.DMA
    covariance, factor_means = pl.pallas_call(
        functools.partial(kernel, n),
        out_shape=(pltpu.VMEM((block, width), f32), pltpu.VMEM((1, width), f32)),
        in_specs=[pl.BlockSpec(memory_space=pl.ANY)],
        out_specs=[pl.BlockSpec(memory_space=pltpu.VMEM)] * 2,
        scratch_shapes=[
            pltpu.VMEM((rows, width), f32),
            pltpu.VMEM((rows, width), f32),
            pltpu.VMEM((rows, 2 * width + width // 2), bf16),
            pltpu.VMEM((rows, 2 * width + width // 2), bf16),
            pltpu.VMEM((tasks, 2, block, wide), f32),
            pltpu.VMEM((tasks, 2, block, wide), f32),
            pltpu.VMEM((tasks, 2, block, wide), f32),
            pltpu.VMEM((tasks, block, wide), f32),
            pltpu.VMEM((tasks, block, wide), f32),
            pltpu.VMEM((tasks, block, wide), f32),
            pltpu.VMEM((2, 3, block, wide), f32),
            pltpu.VMEM((3, block, block), f32),
            pltpu.VMEM((half // 2, block, block), f32),
            pltpu.VMEM((half // 2, block, block), f32),
            pltpu.VMEM((n, 1, width), f32),
            pltpu.VMEM((n, 1, width), f32),
            pltpu.VMEM((1, width), f32),
            pltpu.VMEM((n, 2 * width + width // 2), f32),
            dma((LOADS,)),
            dma((LOADS,)), dma((LOADS,)),
            dma, dma,
            dma((tasks, 2)), dma((tasks, 2)),
            dma((tasks,)), dma((tasks,)),
            dma((tasks,)), dma((2, 3)),
            dma((2,)), dma((3,)),
            dma((half // 2,)), dma((half // 2,)),
            dma((n,)), dma((n,)),
            dma, dma,
        ],
        compiler_params=pltpu.CompilerParams(
            collective_id=0, has_side_effects=True, vmem_limit_bytes=60 * 1024 * 1024
        ),
    )(scenario_pnl)
    return covariance, factor_means.reshape(width)


def solution(mesh):
    n, cores = mesh.shape["scen"], mesh.shape["fac"]

    def body(scenario_pnl):
        rows, width = scenario_pnl.shape
        fits = cores == 2 and n % 16 == 0 and n // 4 == 4 and width % (n * 64) == 0
        if fits and rows % (LOADS * TILE) == 0:
            return by_kernel(n, scenario_pnl)
        return on_device(scenario_pnl)

    return jax.shard_map(
        body,
        mesh=mesh,
        in_specs=(P("scen", "fac"),),
        out_specs=(P("scen", "fac"), P("fac")),
        check_vma=False,
    )
```

time: 68.5 us -> 59.4 us (0.87)
  Pallas kernels: 66.3 us -> 56.8 us
    pallas_call x1, Pallas kernels: 66.3 us -> 56.8 us  [by_kernel(): pl.pallas_call(functools.partial(kernel, n), out_shape=(pltpu.VMEM((block...]
where the time goes in v2:
time: 59.4 us; the launch traced here: 58.8 us
  Pallas kernels  56.8 us (96%)
  local copies, waits for them, and re-layouts  1.39 us (2%)
  between operations  0.64 us (1%)
    pallas_call x1, Pallas kernels, by_kernel(): pl.pallas_call(functools.partial(kernel, n), out_shape=(pltpu.VMEM((block...  56.8 us
    unnamed x2, local copies, waits for them, and re-layouts  1.39 us

profile of v2, /device:TPU:1, one launch (start us, length us, event | category | flops | bytes accessed | tf_op | source)
XLA Modules:
  0.0 58.8 jit_solution(7160703506947618582)
XLA Ops:
  0.6 56.8 %shard_map.30 = (f32[128,1024]{1,0:T(8,128)S(1)}, f32[1,1024]{1,0:T(1,128)S(1)}) custom-call(f32[1024,1024]{1,0:T(8,128)} %x_hbm.1), custom_call_target="tpu_custom_call" | custom-call | tf_op jit(solution)/shard_map/pallas_call | solution.py:401
  57.4 0.8 %copy.5 = f32[128,1024]{1,0:T(8,128)} copy(f32[128,1024]{1,0:T(8,128)S(1)} %get-tuple-element.6) | data formatting | bytes 1048576
  58.2 0.6 %copy.6 = f32[1024]{0:T(1024)} copy(f32[1024]{0:T(1024)S(1)} %bitcast.1) | data formatting | bytes 8192

commit v3 on v2

v3 whole, which is shorter than its diff:
```python
import functools

import jax
import jax.numpy as jnp
from jax import lax
from jax.experimental import pallas as pl
from jax.experimental.pallas import tpu as pltpu
from jax.sharding import PartitionSpec as P

MESH = pl.DeviceIdType.MESH
LOADS = 4
TILE = 64
AHEAD = 2


def block_gram(left, right):
    return lax.dot_general(
        left,
        right,
        (((0,), (0,)), ((), ())),
        precision=lax.Precision.HIGHEST,
        preferred_element_type=jnp.float32,
    )


def on_device(scenario_pnl):
    rows_here = scenario_pnl.shape[0]
    total_rows = rows_here * lax.axis_size("scen")
    local_sums = jnp.sum(scenario_pnl, axis=0)
    total_sums = lax.psum(local_sums, "scen")
    factor_means = total_sums / total_rows
    local_means = local_sums / rows_here
    data = scenario_pnl - local_means[None, :]
    partial_value = block_gram(lax.all_gather(data, "fac", axis=1, tiled=True), data)
    owned = lax.psum_scatter(partial_value, "scen", scatter_dimension=0, tiled=True)
    gathered = lax.all_gather(local_means, ("scen", "fac"), axis=0, tiled=True)
    spread_rows = gathered.reshape(lax.axis_size("scen"), -1)
    deviations = spread_rows - jnp.mean(spread_rows, axis=0, keepdims=True)
    owned_rows = owned.shape[0]
    column_width = owned.shape[1]
    row_part = lax.dynamic_slice_in_dim(
        deviations, lax.axis_index("scen") * owned_rows, owned_rows, 1
    )
    column_part = lax.dynamic_slice_in_dim(
        deviations, lax.axis_index("fac") * column_width, column_width, 1
    )
    owned = owned + rows_here * block_gram(row_part, column_part)
    covariance = owned / (total_rows - 1)
    return (covariance, factor_means)


def kernel(
    n, x_hbm, cov_ref, mean_ref,
    x_vm, other, hi, lo,
    send1, keep1, recv1, send2, recv2, zpair, zland, zsend, zrecv, xrecv, late,
    turned, landed, sums_own, sums_oth, pair_sum, dev_a,
    load_sem, pair_s, pair_r, ps_s, ps_r, s1_s, s1_r, s2_s, s2_r, z_s, z_r, x_s, x_r,
    t_s, t_r, m_s, m_r, mo_s, mo_r,
):
    rows, width = x_hbm.shape
    half = n // 2
    block = width // half
    quads = n // 4
    strip_blocks = half // 2
    wide = AHEAD * block
    rest = (strip_blocks - AHEAD) * block
    extra = 2 * quads
    wrapped = width + width // 2
    total_rows = rows * n

    s = lax.axis_index("scen")
    c = lax.axis_index("fac")
    z, y, x = s // 4, (s // 2) % 2, s % 2
    first = x * (1 - c) + y * c
    second = y * (1 - c) + x * c
    peer1 = s + (1 - 2 * x) * (1 - c) + (2 - 4 * y) * c
    peer2 = s + (2 - 4 * y) * (1 - c) + (1 - 2 * x) * c
    odd, high, own_z = z % 2, z // 2, 1 - (z // 2 - c) * (z // 2 - c)
    inner, twin = odd + high - 2 * odd * high, z + 1 - 2 * odd

    barrier = pltpu.get_barrier_semaphore()
    me = s * 2 + c

    part = rows // LOADS
    loads = []
    for i in range(LOADS):
        at = pl.ds(i * part, part)
        load = pltpu.make_async_copy(x_hbm.at[at], x_vm.at[at], load_sem.at[i])
        load.start()
        loads.append(load)

    for d in range(1, 2 * n):
        p = (me + d) % (2 * n)
        pl.semaphore_signal(barrier, inc=1, device_id=(p // 2, p % 2), device_id_type=MESH)

    def sums_of(ref, start, count, acc):
        def add(i, acc):
            at = pl.multiple_of(start + i * TILE, TILE)
            return acc + jnp.sum(ref[pl.ds(at, TILE), :].reshape(TILE // 8, 8, width), axis=0)

        return lax.fori_loop(0, count // TILE, add, acc)

    acc = jnp.zeros((8, width), jnp.float32)
    for i in range(LOADS):
        loads[i].wait()
        acc = sums_of(x_vm, i * part, part, acc)
    local_sum = jnp.sum(acc, axis=0, keepdims=True)
    sums_own[s] = local_sum
    mid = width // 2

    def split(ref, mean, cols, base, start, count, wrap):
        def body(i, carry):
            at = pl.ds(pl.multiple_of(start + i * TILE, TILE), TILE)
            data = ref[at, cols] - mean
            top = data.astype(jnp.bfloat16)
            low = (data - top.astype(jnp.float32)).astype(jnp.bfloat16)
            to = pl.ds(pl.multiple_of(base, block), data.shape[1])
            hi[at, to] = top
            lo[at, to] = low
            if wrap:
                hi[at, width:wrapped] = top[:, :mid]
                lo[at, width:wrapped] = low[:, :mid]
            return carry

        lax.fori_loop(0, count // TILE, body, 0)

    split(x_vm, local_sum / rows, slice(None), 0, 0, rows, True)

    def gram(left, right):
        return lax.dot_general(
            left, right, (((0,), (0,)), ((), ())), preferred_element_type=jnp.float32
        )

    def slot_of(k):
        mine = (z + 1 - 2 * odd, 3 - 3 * c, 2 - c, z)[k]
        other_half = (3 * c, 1 + c, z + 1 - 2 * odd, z)[k]
        return own_z * mine + (1 - own_z) * other_half

    def slot_late(t):
        across = 2 * (1 - high)
        return (across + 1 - high, across + high, twin, z)[t - quads]

    def slot(t):
        return slot_of(t) if t < quads else slot_late(t)

    def width_of(t):
        return (wide, rest, block)[t // quads]

    def strip(to, px, py):
        r = (to * 4 + py * 2 + px) % half
        own = 1 - (to // 2 - c) * (to // 2 - c)
        return r + (1 - own) * (wrapped // block), r + (1 - own) * c

    def lanes(start, count):
        return pl.ds(pl.multiple_of(start * block, block), count)

    def product(left, right, count):
        rows_at, cols_at = lanes(left, block), lanes(right, count)
        lh, ll = hi[:, rows_at], lo[:, rows_at]
        rh, rl = hi[:, cols_at], lo[:, cols_at]
        return gram(lh, rh) + (gram(lh, rl) + gram(ll, rh))

    def compute(t, side, dst, send=False):
        def body(j, carry):
            b = (1 - second) + j * (2 * second - 1)
            px, py = side * (1 - c) + b * c, b * (1 - c) + side * c
            if t == extra:
                r = py * 2 + px
                late[quads, 0 if send else 1, j, :, :block] = product(r, r + half // 2, block)
            else:
                to = slot_of(t)
                value = product(*strip(to, px, py), wide + rest)
                dst[t, j] = value[:, :wide]
                late[to, 0 if send else 1, j] = value[:, wide:]
            if send:
                stage1(t, j).start()
            return carry

        lax.fori_loop(0, 2, body, 0)

    def remote(src, dst, send, recv, scen, fac):
        return pltpu.make_async_remote_copy(
            src_ref=src, dst_ref=dst, send_sem=send, recv_sem=recv,
            device_id=(scen, fac), device_id_type=MESH,
        )

    def sent(t, j):
        if t < quads:
            return send1.at[t, j]
        return late.at[quads if t == extra else slot_late(t), 0, j, :, :width_of(t)]

    def kept(t, j):
        if t < quads:
            return keep1[t, j]
        return late[quads if t == extra else slot_late(t), 1, j, :, :width_of(t)]

    def stage1(t, j):
        return remote(
            sent(t, j), recv1.at[t, j, :, :width_of(t)], s1_s.at[t // quads // 2], s1_r.at[t, j], peer1, c
        )

    def stage2(t):
        w = width_of(t)
        return remote(send2.at[t, :, :w], recv2.at[t, :, :w], s2_s.at[t // quads // 2], s2_r.at[t], peer2, c)

    def crosses(t):
        if t >= quads:
            return (1, 1, 0)[t - quads], t - quads
        return (1 - own_z, 1, own_z)[t], t - own_z

    def stage3(t):
        w = width_of(t)
        cross, order = crosses(t)
        last = cross * inner
        place = last + cross * (1 - inner) * (2 + order)
        if t < quads:
            src, dst = zpair.at[t], zland.at[place]
        else:
            src, dst = zsend.at[t, :, :w], zrecv.at[place]
        return remote(
            src, dst, z_s.at[t // quads], z_r.at[t // quads, place],
            (last * slot(t) + (1 - last) * twin) * 4 + y * 2 + x, c,
        )

    def from_z(t, place):
        p = t // quads
        to = zrecv.at[place] if p else zland.at[place]
        remote(to, to, z_s.at[p], z_r.at[p, place], s, 1 - c).wait_recv()
        return to[...]

    def relay3(t):
        cross, order = crosses(t)

        @pl.when(cross * inner == 1)
        def _():
            if t < quads:
                zpair[t] = zpair[t] + from_z(t, 2 + order)
            else:
                zsend[t, :, :rest] = zsend[t, :, :rest] + from_z(t, 2 + order)
            stage3(t).start()

    def stage3_extra(e):
        to = 2 * c + e
        place = (z - to + quads - 1) % quads
        return remote(
            zsend.at[extra, :, :block], xrecv.at[place], x_s.at[e], x_r.at[place],
            to * 4 + y * 2 + x, c,
        )

    def with_stage3(t, act, every=False):
        if t == extra:
            for e in range(2):
                pl.when(2 * c + e != z)(act(stage3_extra(e)))
        elif t % quads < quads - 1:
            pl.when((crosses(t)[0] * inner == 0) | every)(act(stage3(t)))

    def relay1(t):
        w = width_of(t)
        if t < quads:
            for j in range(2):
                stage1(t, j).wait_recv()
                zpair[t, j] = keep1[t, j] + recv1[t, j, :, :w]
            if t:
                with_stage3(t, lambda copy: copy.start)
            else:
                pl.when((own_z == 0) & (inner == 0))(stage3(0).start)
            if t == 2:
                pl.when(own_z == 1)(stage3(0).start)
            return
        stage1(t, 0).wait_recv()
        send2[t, :, :w] = kept(t, 0) + recv1[t, 0, :, :w]
        stage2(t).start()

    def join1():
        t = quads - 1
        a, b = from_z(t, 0), from_z(t, 1)
        send2[t, :, :wide] = zpair[t, 0] + a[0] + b[0]
        stage2(t).start()
        zsend[t, :, :wide] = zpair[t, 1] + a[1] + b[1]

    def relay2(t):
        w = width_of(t)
        stage1(t, 1).wait_recv()
        stage2(t).wait_recv()
        zsend[t, :, :w] = kept(t, 1) + recv1[t, 1, :, :w] + recv2[t, :, :w]
        with_stage3(t, lambda copy: copy.start)

    def send_stage(t):
        for j in range(2):
            stage1(t, j).start()

    def pair_copy(i, mine):
        h = own_z * (1 - odd) + (1 - own_z) * c if mine else own_z * (1 - c) + (1 - own_z) * (1 - odd)
        h = h if i < 2 else 1 - h
        at = pl.ds(i % 2 * (rows // 2), rows // 2), pl.ds(pl.multiple_of(h * mid, block), mid)
        return h, remote(x_vm.at[at], other.at[at], pair_s, pair_r.at[i // 2], s, 1 - c)

    def pair_part(half_at):
        h, _ = pair_copy(2 * half_at, False)
        cols = pl.ds(pl.multiple_of(h * mid, block), mid)
        to = other.at[:, cols]
        remote(to, to, pair_s, pair_r.at[half_at], s, 1 - c).wait_recv()
        split(other, pair_sum[:, cols] / rows, cols, wrapped + h * mid, 0, rows, False)

    def mean_copy(d):
        p = (s + d) % n
        return remote(sums_own.at[s], sums_own.at[s], m_s, m_r, p, c)

    pl.semaphore_wait(barrier, 2 * n - 1)
    pair_mean = remote(sums_own.at[s], pair_sum, ps_s, ps_r, s, 1 - c)
    pair_mean.start()
    for i in range(4):
        pair_copy(i, True)[1].start()
    compute(extra, 1 - first, send1, True)
    compute(0, 1 - first, send1, True)
    for d in range(1, n):
        mean_copy(d).start()
    compute(extra, first, keep1)
    compute(0, first, keep1)
    relay1(extra)

    pair_mean.wait_recv()
    pair_part(0)
    compute(1, 1 - first, send1, True)
    compute(1, first, keep1)
    relay1(0)
    pair_part(1)
    compute(2, 1 - first, send1, True)
    relay2(extra)
    compute(2, first, keep1)
    compute(3, 1 - first, send1, True)
    for t in range(quads, 2 * quads):
        send_stage(t)
    relay1(1)
    compute(3, first, keep1)
    relay1(2)
    relay3(0)
    relay1(3)
    relay1(quads)
    most_sums = sums_own.at[pl.ds(0, n - 1)]
    all_means = remote(most_sums, most_sums, m_s, m_r, s, 1 - c)
    all_means.wait_recv()
    swap = remote(sums_own, sums_oth, mo_s, mo_r, s, 1 - c)
    swap.start()
    relay3(1)

    def deviations(ref):
        sums = ref[...].reshape(n, width)
        total = jnp.sum(sums, axis=0, keepdims=True)
        return sums / rows - total / total_rows, total / total_rows

    dev, means = deviations(sums_own)
    mean_ref[...] = means
    dev_a[:, :width] = dev
    dev_a[:, width:wrapped] = dev[:, :mid]
    swap.wait_recv()
    dev_a[:, wrapped:] = deviations(sums_oth)[0]

    r = s % half
    start = r + (1 - own_z) * c

    def put(q, value):
        cov_ref[:, lanes(q % half, block)] = value

    def turn_copy(d):
        return remote(
            turned.at[d], landed.at[d], t_s.at[(d + strip_blocks - 1) // strip_blocks], t_r.at[d],
            c * half + (start + d) % half, own_z * c + (1 - own_z) * (1 - c),
        )

    def mirrored(d, act):
        if d:
            act()
        else:
            pl.when(own_z == 0)(act)

    def finish(p):
        t = p * quads + quads - 1
        w = width_of(t)
        if p:
            arrived = [from_z(t, place) for place in range(2)]
        else:
            stage2(t).wait_recv()
            arrived = [recv2[t, :, :w]]
        left, right = strip(z, x, y)
        right = right + p * AHEAD
        shift = block_gram(dev_a[:, lanes(left, block)], dev_a[:, lanes(right, w)])
        value = zsend[t, :, :w]
        for other_z in arrived:
            value = value + other_z
        value = (value + rows * shift) / (total_rows - 1)
        pieces = piece(p)
        for i, d in enumerate(pieces):
            turned[d] = value[:, i * block:(i + 1) * block].T
            mirrored(d, turn_copy(d).start)
        for i, d in enumerate(pieces):
            put(start + d, value[:, i * block:(i + 1) * block])

    def piece(p):
        return range(AHEAD, strip_blocks) if p else range(AHEAD)

    def land(p):
        for d in piece(p):
            def arrive():
                turn_copy(d).wait_recv()
                put(r - (1 - own_z) * (1 - c) - d + 2 * half, landed[d])

            mirrored(d, arrive)

    def finish_extra():
        @pl.when(own_z == 1)
        def _():
            for place in range(quads - 1):
                remote(
                    zsend.at[extra, :, :block], xrecv.at[place], x_s.at[0], x_r.at[place], s, 1 - c
                ).wait_recv()
            left = y * 2 + x
            shift = block_gram(
                dev_a[:, lanes(left, block)], dev_a[:, lanes(left + half // 2, block)]
            )
            value = zsend[extra, :, :block]
            for place in range(quads - 1):
                value = value + xrecv[place]
            value = (value + rows * shift) / (total_rows - 1)

            @pl.when(odd == 0)
            def _():
                put(r + half // 2, value)

            @pl.when(odd == 1)
            def _():
                put(r + half // 2, value.T)

    relay1(quads + 1)
    relay2(quads)
    relay3(2)
    relay1(quads + 2)
    relay2(quads + 1)
    relay3(quads)
    join1()
    relay1(quads + 3)
    relay2(quads + 2)
    relay3(quads + 1)
    finish(0)
    finish_extra()
    relay2(quads + 3)
    finish(1)
    land(0)
    land(1)

    def sent_bytes(ref, sem):
        remote(ref, ref, sem, ps_r, s, 1 - c).wait_send()

    pair_mean.wait_send()
    swap.wait_send()
    sent_bytes(other, pair_s)
    all_means.wait_send()
    for d in range(min(2, strip_blocks)):
        pl.when((d == 1) | (own_z == 0))(
            functools.partial(
                sent_bytes, landed.at[pl.ds(d, (1, strip_blocks - 1)[d])], t_s.at[d]
            )
        )
    sent_bytes(send1, s1_s.at[0])
    sent_bytes(late.at[pl.ds(0, quads), 1], s1_s.at[0])
    sent_bytes(late.at[quads, 1, :, :, :block], s1_s.at[1])
    sent_bytes(recv2.at[quads - 1, :, :wide], s2_s.at[0])
    sent_bytes(recv2.at[pl.ds(quads, quads), :, :rest], s2_s.at[0])
    sent_bytes(recv2.at[extra, :, :block], s2_s.at[1])
    sent_bytes(zpair.at[pl.ds(0, quads - 1)], z_s.at[0])
    sent_bytes(zsend.at[pl.ds(quads, quads - 1), :, :rest], z_s.at[1])
    with_stage3(extra, lambda copy: copy.wait_send)


def by_kernel(n, scenario_pnl):
    rows, width = scenario_pnl.shape
    half = n // 2
    block = width // half
    wide, rest = AHEAD * block, (half // 2 - AHEAD) * block
    most = max(wide, rest)
    tasks = 2 * (n // 4) + 1
    f32, bf16 = jnp.float32, jnp.bfloat16
    dma = pltpu.SemaphoreType.DMA
    covariance, factor_means = pl.pallas_call(
        functools.partial(kernel, n),
        out_shape=(pltpu.VMEM((block, width), f32), pltpu.VMEM((1, width), f32)),
        in_specs=[pl.BlockSpec(memory_space=pl.ANY)],
        out_specs=[pl.BlockSpec(memory_space=pltpu.VMEM)] * 2,
        scratch_shapes=[
            pltpu.VMEM((rows, width), f32),
            pltpu.VMEM((rows, width), f32),
            pltpu.VMEM((rows, 2 * width + width // 2), bf16),
            pltpu.VMEM((rows, 2 * width + width // 2), bf16),
            pltpu.VMEM((n // 4, 2, block, wide), f32),
            pltpu.VMEM((n // 4, 2, block, wide), f32),
            pltpu.VMEM((tasks, 2, block, most), f32),
            pltpu.VMEM((tasks, block, most), f32),
            pltpu.VMEM((tasks, block, most), f32),
            pltpu.VMEM((n // 4, 2, block, wide), f32),
            pltpu.VMEM((4, 2, block, wide), f32),
            pltpu.VMEM((tasks, block, most), f32),
            pltpu.VMEM((4, block, rest), f32),
            pltpu.VMEM((3, block, block), f32),
            pltpu.VMEM((n // 4 + 1, 2, 2, block, rest), f32),
            pltpu.VMEM((half // 2, block, block), f32),
            pltpu.VMEM((half // 2, block, block), f32),
            pltpu.VMEM((n, 1, width), f32),
            pltpu.VMEM((n, 1, width), f32),
            pltpu.VMEM((1, width), f32),
            pltpu.VMEM((n, 2 * width + width // 2), f32),
            dma((LOADS,)),
            dma, dma((2,)),
            dma, dma,
            dma((2,)), dma((tasks, 2)),
            dma((2,)), dma((tasks,)),
            dma((2,)), dma((2, 4)),
            dma((2,)), dma((3,)),
            dma((2,)), dma((half // 2,)),
            dma, dma,
            dma, dma,
        ],
        compiler_params=pltpu.CompilerParams(
            collective_id=0, has_side_effects=True, vmem_limit_bytes=60 * 1024 * 1024
        ),
    )(scenario_pnl)
    return covariance, factor_means.reshape(width)


def solution(mesh):
    n, cores = mesh.shape["scen"], mesh.shape["fac"]

    def body(scenario_pnl):
        rows, width = scenario_pnl.shape
        fits = cores == 2 and n % 16 == 0 and n // 4 == 4 and width % (n * 64) == 0
        if fits and rows % (LOADS * TILE) == 0:
            return by_kernel(n, scenario_pnl)
        return on_device(scenario_pnl)

    return jax.shard_map(
        body,
        mesh=mesh,
        in_specs=(P("scen", "fac"),),
        out_specs=(P("scen", "fac"), P("fac")),
        check_vma=False,
    )
```

time: 59.4 us -> 56.7 us (0.955)
  the two profiles are of different devices: /device:TPU:1 before, /device:TPU:0 now
where the time goes in v3:
time: 56.7 us; the launch traced here: 56.6 us
  Pallas kernels  54.5 us (96%)
  local copies, waits for them, and re-layouts  1.39 us (2%)
  between operations  0.64 us (1%)
    pallas_call x1, Pallas kernels, by_kernel(): pl.pallas_call(functools.partial(kernel, n), out_shape=(pltpu.VMEM((block...  54.5 us
    unnamed x2, local copies, waits for them, and re-layouts  1.39 us

profile of v3, /device:TPU:0, one launch (start us, length us, event | category | flops | bytes accessed | tf_op | source)
XLA Modules:
  0.0 56.6 jit_solution(11651806334237329545)
XLA Ops:
  0.6 54.5 %shard_map.30 = (f32[128,1024]{1,0:T(8,128)S(1)}, f32[1,1024]{1,0:T(1,128)S(1)}) custom-call(f32[1024,1024]{1,0:T(8,128)} %x_hbm.1), custom_call_target="tpu_custom_call" | custom-call | tf_op jit(solution)/shard_map/pallas_call | solution.py:484
  55.2 0.8 %copy.5 = f32[128,1024]{1,0:T(8,128)} copy(f32[128,1024]{1,0:T(8,128)S(1)} %get-tuple-element.6) | data formatting | bytes 1048576
  56.0 0.6 %copy.6 = f32[1024]{0:T(1024)} copy(f32[1024]{0:T(1024)S(1)} %bitcast.1) | data formatting | bytes 8192

commit v4 on v3

--- a/solution.py
+++ b/solution.py
@@ -324,9 +324,9 @@
     compute(1, 1 - first, send1, True)
     compute(1, first, keep1)
     relay1(0)
+    relay2(extra)
     pair_part(1)
     compute(2, 1 - first, send1, True)
-    relay2(extra)
     compute(2, first, keep1)
     compute(3, 1 - first, send1, True)
     for t in range(quads, 2 * quads):

time: 56.7 us -> 55.8 us (0.984)
  the two profiles are of different devices: /device:TPU:0 before, /device:TPU:1 now
where the time goes in v4:
time: 55.8 us; the launch traced here: 55.4 us
  Pallas kernels  53.3 us (96%)
  local copies, waits for them, and re-layouts  1.39 us (2%)
  between operations  0.64 us (1%)
    pallas_call x1, Pallas kernels, by_kernel(): pl.pallas_call(functools.partial(kernel, n), out_shape=(pltpu.VMEM((block...  53.3 us
    unnamed x2, local copies, waits for them, and re-layouts  1.39 us

profile of v4, /device:TPU:1, one launch (start us, length us, event | category | flops | bytes accessed | tf_op | source)
XLA Modules:
  0.0 55.4 jit_solution(9628019725466731848)
XLA Ops:
  0.6 53.3 %shard_map.30 = (f32[128,1024]{1,0:T(8,128)S(1)}, f32[1,1024]{1,0:T(1,128)S(1)}) custom-call(f32[1024,1024]{1,0:T(8,128)} %x_hbm.1), custom_call_target="tpu_custom_call" | custom-call | tf_op jit(solution)/shard_map/pallas_call | solution.py:484
  54.0 0.8 %copy.5 = f32[128,1024]{1,0:T(8,128)} copy(f32[128,1024]{1,0:T(8,128)S(1)} %get-tuple-element.6) | data formatting | bytes 1048576
  54.8 0.6 %copy.6 = f32[1024]{0:T(1024)} copy(f32[1024]{0:T(1024)S(1)} %bitcast.1) | data formatting | bytes 8192

commit v5 on v4

--- a/solution.py
+++ b/solution.py
@@ -312,13 +312,12 @@
     for i in range(4):
         pair_copy(i, True)[1].start()
     compute(extra, 1 - first, send1, True)
-    compute(0, 1 - first, send1, True)
     for d in range(1, n):
         mean_copy(d).start()
+    compute(0, 1 - first, send1, True)
+    compute(0, first, keep1)
     compute(extra, first, keep1)
-    compute(0, first, keep1)
     relay1(extra)
-
     pair_mean.wait_recv()
     pair_part(0)
     compute(1, 1 - first, send1, True)
@@ -334,14 +333,14 @@
     relay1(1)
     compute(3, first, keep1)
     relay1(2)
-    relay3(0)
     relay1(3)
-    relay1(quads)
     most_sums = sums_own.at[pl.ds(0, n - 1)]
     all_means = remote(most_sums, most_sums, m_s, m_r, s, 1 - c)
     all_means.wait_recv()
     swap = remote(sums_own, sums_oth, mo_s, mo_r, s, 1 - c)
     swap.start()
+    relay1(quads + 0)
+    relay3(0)
     relay3(1)
 
     def deviations(ref):
@@ -432,11 +431,11 @@
                 put(r + half // 2, value.T)
 
     relay1(quads + 1)
-    relay2(quads)
+    relay2(quads + 0)
     relay3(2)
     relay1(quads + 2)
     relay2(quads + 1)
-    relay3(quads)
+    relay3(quads + 0)
     join1()
     relay1(quads + 3)
     relay2(quads + 2)

time: 55.8 us -> 55.5 us (level)
  no operation moved by 1% of the time
where the time goes in v5:
time: 55.5 us; the launch traced here: 55 us
  Pallas kernels  53 us (95%)
  local copies, waits for them, and re-layouts  1.39 us (3%)
  between operations  0.64 us (1%)
    pallas_call x1, Pallas kernels, by_kernel(): pl.pallas_call(functools.partial(kernel, n), out_shape=(pltpu.VMEM((block...  53 us
    unnamed x2, local copies, waits for them, and re-layouts  1.39 us

profile of v5, /device:TPU:1, one launch (start us, length us, event | category | flops | bytes accessed | tf_op | source)
XLA Modules:
  0.0 55.0 jit_solution(4256216500299480123)
XLA Ops:
  0.6 53.0 %shard_map.30 = (f32[128,1024]{1,0:T(8,128)S(1)}, f32[1,1024]{1,0:T(1,128)S(1)}) custom-call(f32[1024,1024]{1,0:T(8,128)} %x_hbm.1), custom_call_target="tpu_custom_call" | custom-call | tf_op jit(solution)/shard_map/pallas_call | solution.py:483
  53.6 0.8 %copy.5 = f32[128,1024]{1,0:T(8,128)} copy(f32[128,1024]{1,0:T(8,128)S(1)} %get-tuple-element.6) | data formatting | bytes 1048576
  54.4 0.6 %copy.6 = f32[1024]{0:T(1024)} copy(f32[1024]{0:T(1024)S(1)} %bitcast.1) | data formatting | bytes 8192
